TPU v7x, 64 devices: a 2x2x8 block of a 4x4x8 slice. The times are simulated.
64 devices in a mesh: dp: 8 (over x, y, core), tp: 8 (over z).
Axes of the slice: x: 2, y: 2, z: 8, core: 2. Of those that a mesh axis runs over, the one named last changes fastest.
The devices are a block of a 4x4x8 slice.
Arguments:
- x: bfloat16 [16384, 4096], P('dp'), parts along dimension 0
- dy: bfloat16 [16384, 4096], P('dp'), parts along dimension 0
- gate: bfloat16 [16384, 10240], P('dp', 'tp'), parts along dimension 0
- up: bfloat16 [16384, 10240], P('dp', 'tp'), parts along dimension 0
- w_gate: bfloat16 [4096, 10240], P(None, 'tp')
- w_up: bfloat16 [4096, 10240], P(None, 'tp')
- w_down: bfloat16 [10240, 4096], P('tp')
Outputs:
- output 1: bfloat16 [16384, 4096], P('dp'), parts along dimension 0
- output 2: bfloat16 [32768, 10240], P('dp', 'tp'), parts along dimension 0
- output 3: bfloat16 [32768, 10240], P('dp', 'tp'), parts along dimension 0
- output 4: bfloat16 [81920, 4096], P(('dp', 'tp')), parts along dimension 0
There are 8 independent parts. A program takes and returns all parts, laid end to end along the dimension named above; an argument that names none is the same for every part.
All inputs are finite; a program needn't handle non-finite values.
Results may differ from a plain program's by a relative error of at most 0.012.
Values are sent between devices in bfloat16 or wider.
A program may use at most 768 MiB of HBM per device.

v0:
```python
import jax
import jax.numpy as jnp
from jax import lax
from jax.sharding import PartitionSpec as P


def act(gate, up):
    return jax.nn.gelu(gate) * up


def solution(mesh):
    def step(x, dy, gate, up, w_gate, w_up, w_down):
        hidden, back = jax.vjp(act, gate.astype(jnp.float32), up.astype(jnp.float32))
        d_hidden = jnp.dot(dy, w_down.T, preferred_element_type=jnp.float32)
        d_gate, d_up = (g.astype(jnp.bfloat16) for g in back(d_hidden))
        term = jnp.dot(d_gate, w_gate.T, preferred_element_type=jnp.float32) + jnp.dot(d_up, w_up.T, preferred_element_type=jnp.float32)
        dx = lax.psum(term.astype(jnp.bfloat16), "tp")
        dw_gate = jnp.dot(x.T, d_gate, preferred_element_type=jnp.float32)
        dw_up = jnp.dot(x.T, d_up, preferred_element_type=jnp.float32)
        dw_down = jnp.dot(hidden.astype(jnp.bfloat16).T, dy, preferred_element_type=jnp.float32)
        return dx, *(g.astype(jnp.bfloat16) for g in (dw_gate, dw_up, dw_down))

    tokens, columns, rows = P("dp", None), P(None, "tp"), P("tp", None)
    return jax.shard_map(
        step,
        mesh=mesh,
        in_specs=(tokens, tokens, P("dp", "tp"), P("dp", "tp"), columns, columns, rows),
        out_specs=(tokens, P("dp", "tp"), P("dp", "tp"), P(("dp", "tp"), None)),
        check_vma=False,
    )
```

profile of v0, /device:TPU:21, one launch (start us, length us, event | category | flops | bytes accessed | tf_op | source)
XLA Modules:
  0.0 470.0 jit_solution(1074908950645164616)
XLA Ops:
  7.2 0.1 all-reduce.2.cloned.1.call-start
  7.2 36.7 %fusion.6 = (bf16[2048,1280]{1,0:T(8,128)(2,1)}, f32[2048,1280]{1,0:T(8,128)}) fusion(bf16[2048,1280]{1,0:T(8,128)(2,1)} %param.9, bf16[2048,1280]{1,0:T(8,128)(2,1)} %param.10, bf16[2048,4096]{1,0:T(8,128)(2,1)} %param.8, bf16[1280,4096]{1,0:T(8,128)(2,1)} %param.13), kind=kOutput, calls=%fused_computation.17 | convolution fusion | flops 21535129600 | bytes 53477376 | tf_op jit(solution)/shard_map/dot_general | solution.py:14
  44.0 29.1 %fusion.21 = f32[2048,4096]{1,0:T(8,128)} fusion(bf16[2048,1280]{1,0:T(8,128)(2,1)} %get-tuple-element.8, bf16[4096,1280]{1,0:T(8,128)(2,1)} %param.11), kind=kOutput, calls=%fused_computation.32 | convolution fusion | flops 21474836480 | bytes 49283072 | tf_op jit(solution)/shard_map/dot_general | solution.py:16
  73.1 32.9 %add_convert_fusion = bf16[2048,4096]{1,0:T(8,128)(2,1)} fusion(f32[2048,4096]{1,0:T(8,128)} %fusion.21, bf16[4096,1280]{1,0:T(8,128)(2,1)} %param.12, f32[2048,1280]{1,0:T(8,128)} %get-tuple-element.9, bf16[2048,1280]{1,0:T(8,128)(2,1)} %param.9), kind=kOutput, calls=%fused_computation | convolution fusion | flops 21520449536 | bytes 76546048 | tf_op jit(solution)/shard_map/dot_general | solution.py:16
  106.0 0.1 all-reduce.2.cloned.1.call-update
  106.1 27.9 %fusion.1 = bf16[4096,1280]{0,1:T(8,128)(2,1)} fusion(bf16[2048,1280]{1,0:T(8,128)(2,1)} %get-tuple-element.8, bf16[2048,4096]{1,0:T(8,128)(2,1)} %param.7), kind=kOutput, calls=%fused_computation.12 | convolution fusion | flops 21480079360 | bytes 32505856 | tf_op jit(solution)/shard_map/dot_general | solution.py:18
  134.0 15.0 %copy.11 = bf16[4096,1280]{1,0:T(8,128)(2,1)} copy(bf16[4096,1280]{0,1:T(8,128)(2,1)} %fusion.1) | data formatting | bytes 20971520
  149.1 42.4 %fusion.2 = bf16[4096,1280]{0,1:T(8,128)(2,1)} fusion(bf16[2048,4096]{1,0:T(8,128)(2,1)} %param.7, f32[2048,1280]{1,0:T(8,128)} %get-tuple-element.9, bf16[2048,1280]{1,0:T(8,128)(2,1)} %param.9), kind=kOutput, calls=%fused_computation.13 | convolution fusion | flops 21508915200 | bytes 42991616 | tf_op jit(solution)/shard_map/dot_general | solution.py:19
  191.4 15.0 %copy.12 = bf16[4096,1280]{1,0:T(8,128)(2,1)} copy(bf16[4096,1280]{0,1:T(8,128)(2,1)} %fusion.2) | data formatting | bytes 20971520
  206.5 42.7 %convolution_convert_fusion = bf16[1280,4096]{1,0:T(8,128)(2,1)} fusion(bf16[2048,4096]{1,0:T(8,128)(2,1)} %param.8, bf16[2048,1280]{1,0:T(8,128)(2,1)} %param.10, bf16[2048,1280]{1,0:T(8,128)(2,1)} %param.9), kind=kOutput, calls=%fused_computation.6 | convolution fusion | flops 21511536640 | bytes 37748736 | tf_op jit(solution)/shard_map/dot_general | solution.py:20
  249.2 199.9 %all-reduce.2.cloned.1.call-done = bf16[2048,4096]{1,0:T(8,128)(2,1)} async-done(((bf16[2048,4096]{1,0:T(8,128)(2,1)}), bf16[2048,4096]{1,0:T(8,128)(2,1)}) %all-reduce.2.cloned.1.call-update) | async-done | bytes 16777232 | tf_op jit(solution)/shard_map/psum | solution.py:17
  449.1 14.1 %copy.14 = bf16[2048,4096]{1,0:T(8,128)(2,1)} copy(bf16[2048,4096]{1,0:T(8,128)(2,1)} %all-reduce.2.cloned.1.call-done) | data formatting | bytes 33554432
Async XLA Ops:
  7.2 441.9 %all-reduce.2.cloned.1.call-start = ((), (), s32[]{:S(2)}) async-start(), calls=%async_computation | async-start | bytes 33554432 | tf_op jit(solution)/shard_map/psum | solution.py:17
Sparse Core Ops, SparseCore 0:
  106.2 342.8 all-reduce.1
where the time goes:
time: 471 us; the launch traced here: 470 us
  matrix products  212 us (45%)
  waiting for transfers between devices  200 us (42%)
  local copies, waits for them, and re-layouts  44.1 us (9%)
  between operations  14.1 us (3%)
    psum x1, waiting for transfers between devices, step(): dx = lax.psum(term.astype(jnp.bfloat16), 'tp')  200 us
    unnamed x3, local copies, waits for them, and re-layouts  44.1 us
    dot_general x1, matrix products, step(): jnp.dot(hidden.astype(jnp.bfloat16).T, dy, preferred_element_type=jnp.flo...  42.7 us
    dot_general x1, matrix products, step(): dw_up = jnp.dot(x.T, d_up, preferred_element_type=jnp.float32)  42.4 us
    dot_general x1, matrix products, step(): d_hidden = jnp.dot(dy, w_down.T, preferred_element_type=jnp.float32)  36.7 us
    dot_general x1, matrix products, step(): jnp.dot(d_up, w_up.T, preferred_element_type=jnp.float32)  32.9 us
    dot_general x1, matrix products, step(): jnp.dot(d_gate, w_gate.T, preferred_element_type=jnp.float32)  29.1 us
    dot_general x1, matrix products, step(): dw_gate = jnp.dot(x.T, d_gate, preferred_element_type=jnp.float32)  27.9 us
  transfers between devices with their start and end apart: 1, of which 1 were waited for; matrix products, arithmetic and copies ran while one was open for 30% of the time, Pallas kernels for 0%

commit v1 on v0

v1 whole, which is shorter than its diff:
```python
import functools

import jax
import jax.numpy as jnp
from jax import lax
from jax.experimental import pallas as pl
from jax.experimental.pallas import tpu as pltpu
from jax.sharding import PartitionSpec as P

MESH = pl.DeviceIdType.MESH
CUTS = 4
FB = 256
TW = 512
NT = (((1,), (1,)), ((), ()))
NN = (((1,), (0,)), ((), ()))


def act(gate, up):
    return jax.nn.gelu(gate) * up


def dot(a, b, dims):
    return lax.dot_general(a, b, dims, preferred_element_type=jnp.float32)


def kernel(
    n, x, dy, gate, up, wg, wu, wd, dx, dwg, dwu, dwd, dg, du, hid,
    wv, wdv, slot, own, dyv, guv, dblk, acc, stx, sty,
    rs_s, rs_r, ag_s, ag_r, ld, wb, wl, lo, tl, so,
):
    bf16 = jnp.bfloat16
    rows, D = x.shape
    F = gate.shape[1]
    J = CUTS
    B, W = rows // n, D // J
    H = B // 2
    NF = F // FB
    S = n - 1
    me = lax.axis_index("tp")
    nbr = (lax.rem(me + 1, n), lax.rem(me + n - 1, n))

    def block(d, t):
        return lax.rem(me + 2 * n - 1 - t, n) if d == 0 else lax.rem(me + 1 + t, n)

    def held(d, a):
        return lax.rem(me + n - a, n) if d == 0 else lax.rem(me + a, n)

    def at(b, d):
        return pl.ds(pl.multiple_of(b * B + d * H, H), H)

    def cut(j):
        return pl.ds(pl.multiple_of(j * W, W), W)

    def remote(src, dst, s, r, d):
        return pltpu.make_async_remote_copy(
            src_ref=src, dst_ref=dst, send_sem=s, recv_sem=r,
            device_id={"tp": nbr[d]}, device_id_type=MESH,
        )

    def rs_copy(d, t, j, first=False):
        src = own.at[d, j] if first else slot.at[d, t - 1, j]
        return remote(src, slot.at[d, t, j], rs_s.at[d, t, j], rs_r.at[d, t, j], d)

    def ag_copy(d, a, j, first=False):
        ref = dx.at[at(held(d, a), d), cut(j)]
        src = slot.at[d, n - 2, j] if first else ref
        return remote(src, ref, ag_s.at[d, a, j], ag_r.at[d, a, j], d)

    def mine(d, j):
        return pltpu.make_async_copy(
            slot.at[d, n - 2, j], dx.at[at(me, d), cut(j)], lo.at[d, j]
        )

    def loads(t, buf):
        out = []
        for d in range(2):
            r, v = at(block(d, t), d), pl.ds(d * H, H)
            out.append((dy.at[r, :], dyv.at[buf, v, :]))
            out.append((gate.at[r, :], guv.at[buf, 0, v, :]))
            out.append((up.at[r, :], guv.at[buf, 1, v, :]))
        return [
            pltpu.make_async_copy(s, v, ld.at[buf, i]) for i, (s, v) in enumerate(out)
        ]

    def stores(t, buf):
        out = []
        for d in range(2):
            r, v = at(block(d, t), d), pl.ds(d * H, H)
            for i, ref in enumerate((dg, du, hid)):
                out.append((dblk.at[buf, i, v, :], ref.at[r, :]))
        return [
            pltpu.make_async_copy(v, s, wb.at[buf, i]) for i, (v, s) in enumerate(out)
        ]

    def down(i):
        r = pl.ds(i * FB, FB)
        return pltpu.make_async_copy(wd.at[r, :], wdv.at[r, :], wl.at[0, i])

    def weights(j):
        r = pl.ds(j * W, W)
        return (
            pltpu.make_async_copy(wg.at[r, :], wv.at[0, r, :], wl.at[1, j]),
            pltpu.make_async_copy(wu.at[r, :], wv.at[1, r, :], wl.at[2, j]),
        )

    def gradients(buf, i):
        c = pl.ds(pl.multiple_of(i * FB, FB), FB)
        back_in = dot(dyv[buf], wdv[c, :], NT)
        g, u = guv[buf, 0, :, c].astype(jnp.float32), guv[buf, 1, :, c].astype(jnp.float32)
        h, back = jax.vjp(act, g, u)
        d_g, d_u = back(back_in)
        dblk[buf, 0, :, c] = d_g.astype(bf16)
        dblk[buf, 1, :, c] = d_u.astype(bf16)
        dblk[buf, 2, :, c] = h.astype(bf16)

    def term(buf, j):
        r = cut(j)
        return dot(dblk[buf, 0], wv[0, r, :], NT) + dot(dblk[buf, 1], wv[1, r, :], NT)

    for c in loads(0, 0):
        c.start()
    for i in range(NF):
        down(i).start()

    barrier = pltpu.get_barrier_semaphore()
    for d in range(2):
        pl.semaphore_signal(barrier, inc=1, device_id={"tp": nbr[d]}, device_id_type=MESH)

    for c in loads(0, 0):
        c.wait()
    for i in range(NF):
        down(i).wait()
        for j in range(J):
            if min(j + 1, NF - 1) == i:
                for c in weights(j):
                    c.start()
        gradients(0, i)
    for c in stores(0, 0):
        c.start()
    for c in loads(1, 1):
        c.start()
    for j in range(J):
        for c in weights(j):
            c.wait()
        part = term(0, j).astype(bf16)
        own[0, j] = part[:H]
        own[1, j] = part[H:]
        if j == 0:
            pl.semaphore_wait(barrier, 2)
        for d in range(2):
            rs_copy(d, 0, j, first=True).start()

    def step(t, carry):
        buf = lax.rem(t, 2)
        for c in loads(t, buf):
            c.wait()

        @pl.when(t >= 2)
        def _():
            for c in stores(t - 2, buf):
                c.wait()

        @pl.when(t < n - 1)
        def _():
            for c in loads(t + 1, 1 - buf):
                c.start()

        def hidden_part(i, carry):
            gradients(buf, i)
            return carry

        lax.fori_loop(0, NF, hidden_part, 0)
        for c in stores(t, buf):
            c.start()

        def piece(j, carry):
            acc[...] = term(buf, j)
            for d in range(2):
                here = slot.at[d, t - 1, j]
                remote(here, here, rs_s.at[d, t - 1, j], rs_r.at[d, t - 1, j], d).wait_recv()
                total = slot[d, t - 1, j].astype(jnp.float32) + acc[pl.ds(d * H, H), :]
                slot[d, t - 1, j] = total.astype(bf16)

            @pl.when(t < n - 1)
            def _():
                for d in range(2):
                    rs_copy(d, t, j).start()

            @pl.when(t == n - 1)
            def _():
                for d in range(2):
                    ag_copy(d, 0, j, first=True).start()
                    mine(d, j).start()

            return carry

        lax.fori_loop(0, J, piece, 0)
        return carry

    lax.fori_loop(1, n, step, 0)

    for t in (n - 2, n - 1):
        for c in stores(t, t % 2):
            c.wait()
    whole = (
        pltpu.make_async_copy(dg, wv.at[0, pl.ds(0, rows), :], wl.at[0, 0]),
        pltpu.make_async_copy(du, wv.at[0, pl.ds(rows, rows), :], wl.at[1, 0]),
        pltpu.make_async_copy(hid, wv.at[1, pl.ds(0, rows), :], wl.at[2, 0]),
    )
    NX = D // TW
    U, K = 3 * NX, S * J

    def tile_ref(s):
        return wv.at[1, pl.ds(rows, rows), pl.ds(pl.multiple_of(s * TW, TW), TW)]

    def tile(T, start):
        s = lax.rem(T, 2)

        @pl.when(T < NX)
        def _():
            c = pltpu.make_async_copy(
                x.at[:, pl.ds(pl.multiple_of(T * TW, TW), TW)], tile_ref(s), tl.at[s]
            )
            c.start() if start else c.wait()

        @pl.when((T >= NX) & (T < 2 * NX))
        def _():
            c = pltpu.make_async_copy(
                dy.at[:, pl.ds(pl.multiple_of((T - NX) * TW, TW), TW)], tile_ref(s), tl.at[s]
            )
            c.start() if start else c.wait()

    def out_x(i, g, f, p):
        r, c = pl.ds(pl.multiple_of(i * TW, TW), TW), pl.ds(pl.multiple_of(f * FB, FB), FB)
        return pltpu.make_async_copy(stx.at[p], (dwg, dwu)[g].at[r, c], so.at[0, p])

    def out_y(i, f, p):
        r, c = pl.ds(pl.multiple_of(f * FB, FB), FB), pl.ds(pl.multiple_of(i * TW, TW), TW)
        return pltpu.make_async_copy(sty.at[p], dwd.at[r, c], so.at[1, p])

    def unit_x(k):
        i, g = k // 2, lax.rem(k, 2)
        s = lax.rem(i, 2)

        @pl.when(g == 0)
        def _():
            tile(i, False)
            tile(i + 1, True)

            def turn(q, carry):
                r = pl.ds(pl.multiple_of(q * FB, FB), FB)
                wdv[pl.ds(0, TW), r] = wv[
                    1, pl.ds(pl.multiple_of(rows + q * FB, FB), FB),
                    pl.ds(pl.multiple_of(s * TW, TW), TW),
                ].T
                return carry

            lax.fori_loop(0, rows // FB, turn, 0)

        def part(f, carry):
            count = k * NF + f
            p = lax.rem(count, 2)
            res = dot(
                wdv[pl.ds(0, TW), pl.ds(0, rows)],
                wv[0, pl.ds(pl.multiple_of(g * rows, rows), rows),
                   pl.ds(pl.multiple_of(f * FB, FB), FB)],
                NN,
            ).astype(bf16)

            @pl.when(count >= 2)
            def _():
                out_x(0, 0, 0, p).wait()

            stx[p] = res
            for v in range(2):
                @pl.when(g == v)
                def _():
                    out_x(i, v, f, p).start()

            return carry

        lax.fori_loop(0, NF, part, 0)

    def unit_y(k):
        i = k - 2 * NX
        s = lax.rem(i + NX, 2)

        @pl.when(i == 0)
        def _():
            def turn(q, carry):
                r = pl.ds(pl.multiple_of(q * FB, FB), FB)
                wdv[:, pl.ds(pl.multiple_of(rows + q * FB, FB), FB)] = wv[1, r, :].T
                return carry

            lax.fori_loop(0, rows // FB, turn, 0)

        tile(i + NX, False)
        tile(i + NX + 1, True)

        def part(f, carry):
            count = i * NF + f
            p = lax.rem(count, 2)
            res = dot(
                wdv[pl.ds(pl.multiple_of(f * FB, FB), FB), pl.ds(rows, rows)],
                wv[1, pl.ds(rows, rows), pl.ds(pl.multiple_of(s * TW, TW), TW)],
                NN,
            ).astype(bf16)

            @pl.when(count >= 2)
            def _():
                out_y(0, 0, p).wait()

            sty[p] = res
            out_y(i, f, p).start()
            return carry

        lax.fori_loop(0, NF, part, 0)

    for c in whole:
        c.start()
    tile(0, True)
    for c in whole:
        c.wait()

    def tick(k, carry):
        @pl.when(k < K)
        def _():
            a = k // J + 1
            j = lax.rem(k, J)
            for d in range(2):
                ag_copy(d, a - 1, j).wait_recv()

            @pl.when(a < S)
            def _():
                for d in range(2):
                    ag_copy(d, a, j).start()

        @pl.when(k < 2 * NX)
        def _():
            unit_x(k)

        @pl.when((k >= 2 * NX) & (k < U))
        def _():
            unit_y(k)

        return carry

    lax.fori_loop(0, max(U, K), tick, 0)

    for p in range(2):
        out_x(0, 0, 0, p).wait()
        out_y(0, 0, p).wait()

    def drain(t, carry):
        def one(j, carry):
            for d in range(2):
                remote(slot.at[d, 0, j], slot.at[d, t, j], rs_s.at[d, t, j], rs_r.at[d, t, j], d).wait_send()
                ag_copy(d, t, j).wait_send()
            return carry

        return lax.fori_loop(0, J, one, carry)

    lax.fori_loop(0, n - 1, drain, 0)
    for d in range(2):
        for j in range(J):
            mine(d, j).wait()


def solution(mesh):
    n = mesh.shape["tp"]

    def step(x, dy, gate, up, w_gate, w_up, w_down):
        rows, D = x.shape
        F = gate.shape[1]
        J, B, W = CUTS, rows // n, D // CUTS
        H = B // 2
        bf16 = jnp.bfloat16
        any_ = pl.BlockSpec(memory_space=pl.ANY)
        like = lambda *s: jax.ShapeDtypeStruct(s, bf16)
        dma = pltpu.SemaphoreType.DMA
        out = pl.pallas_call(
            functools.partial(kernel, n),
            out_shape=(
                like(rows, D), like(D, F), like(D, F), like(F, D),
                like(rows, F), like(rows, F), like(rows, F),
            ),
            in_specs=[any_] * 7,
            out_specs=[any_] * 7,
            scratch_shapes=[
                pltpu.VMEM((2, D, F), bf16),
                pltpu.VMEM((F, D), bf16),
                pltpu.VMEM((2, n - 1, J, H, W), bf16),
                pltpu.VMEM((2, J, H, W), bf16),
                pltpu.VMEM((2, B, D), bf16),
                pltpu.VMEM((2, 2, B, F), bf16),
                pltpu.VMEM((2, 3, B, F), bf16),
                pltpu.VMEM((B, W), jnp.float32),
                pltpu.VMEM((2, TW, FB), bf16),
                pltpu.VMEM((2, FB, TW), bf16),
                dma((2, n - 1, J)), dma((2, n - 1, J)),
                dma((2, n - 1, J)), dma((2, n - 1, J)),
                dma((2, 6)), dma((2, 6)), dma((3, max(J, F // FB))),
                dma((2, J)), dma((2,)), dma((2, 2)),
            ],
            compiler_params=pltpu.CompilerParams(
                collective_id=0, has_side_effects=True, vmem_limit_bytes=67043328
            ),
            name="mlp_back",
        )(x, dy, gate, up, w_gate, w_up, w_down)
        return out[:4]

    tokens, columns, rows = P("dp", None), P(None, "tp"), P("tp", None)
    return jax.shard_map(
        step,
        mesh=mesh,
        in_specs=(tokens, tokens, P("dp", "tp"), P("dp", "tp"), columns, columns, rows),
        out_specs=(tokens, P("dp", "tp"), P("dp", "tp"), P(("dp", "tp"), None)),
        check_vma=False,
    )
```

time: 471 us -> 382 us (0.81)
  Pallas kernels: 0 us -> 339 us
  matrix products: 212 us -> 0 us
  waiting for transfers between devices: 200 us -> 0 us
  between operations: 14.1 us -> 0.64 us
    pallas_call x0 -> x1, Pallas kernels: none -> 339 us  [step(): pl.pallas_call(functools.partial(kernel, n), out_shape=(like(rows, D), li...]
    dot_general x6 -> x0, matrix products: 212 us -> none  [the longest x1 42.7 us: step(): jnp.dot(hidden.astype(jnp.bfloat16).T, dy, preferred_element_type=jnp.flo...]
    psum x1 -> x0, waiting for transfers between devices: 200 us -> none  [step(): dx = lax.psum(term.astype(jnp.bfloat16), 'tp')]
    unnamed x3 -> x4, local copies, waits for them, and re-layouts: 44.1 us -> 41.2 us
  transfers between devices with their start and end apart: 1 -> 0, of which waited for: 1 -> 0; matrix products, arithmetic and copies ran while one was open for 30% -> 0% of each run, Pallas kernels for 0% -> 0%
where the time goes in v1:
time: 382 us; the launch traced here: 381 us
  Pallas kernels  339 us (89%)
  local copies, waits for them, and re-layouts  41.2 us (11%)
    pallas_call x1, Pallas kernels, step(): pl.pallas_call(functools.partial(kernel, n), out_shape=(like(rows, D), li...  339 us
    unnamed x4, local copies, waits for them, and re-layouts  41.2 us

profile of v1, /device:TPU:21, one launch (start us, length us, event | category | flops | bytes accessed | tf_op | source)
XLA Modules:
  0.0 381.2 jit_solution(18105032236042266328)
XLA Ops:
  0.6 339.3 %mlp_back.1 = (bf16[2048,4096]{1,0:T(8,128)(2,1)}, bf16[4096,1280]{1,0:T(8,128)(2,1)}, bf16[4096,1280]{1,0:T(8,128)(2,1)}, bf16[1280,4096]{1,0:T(8,128)(2,1)}, b...) custom-call(bf16[2048,4096]{1,0:T(8,128)(2,1)} %x.1, bf16[2048,4096]{1,0:T(8,128)(2,1)} %dy.1, ...), custom_call_target="tpu_custom_call" | custom-call | tf_op jit(solution)/shard_map/mlp_back/pallas_call | solution.py:381
  340.0 14.1 %copy.15 = bf16[2048,4096]{1,0:T(8,128)(2,1)} copy(bf16[2048,4096]{1,0:T(8,128)(2,1)} %get-tuple-element.16) | data formatting | bytes 33554432
  354.0 8.7 %copy.16 = bf16[4096,1280]{1,0:T(8,128)(2,1)} copy(bf16[4096,1280]{1,0:T(8,128)(2,1)} %get-tuple-element.17) | data formatting | bytes 20971520
  362.8 8.7 %copy.17 = bf16[4096,1280]{1,0:T(8,128)(2,1)} copy(bf16[4096,1280]{1,0:T(8,128)(2,1)} %get-tuple-element.18) | data formatting | bytes 20971520
  371.5 9.7 %copy.18 = bf16[1280,4096]{1,0:T(8,128)(2,1)} copy(bf16[1280,4096]{1,0:T(8,128)(2,1)} %get-tuple-element.19) | data formatting | bytes 20971520

commit v2 on v1

v2 whole, which is shorter than its diff:
```python
import functools

import jax
import jax.numpy as jnp
from jax import lax
from jax.experimental import pallas as pl
from jax.experimental.pallas import tpu as pltpu
from jax.sharding import PartitionSpec as P


MESH = pl.DeviceIdType.MESH
CUTS = 4
FB = 256
TW = 512
TAIL = 2
PARTS = 2
COPY_FLOPS = 600
NT = (((1,), (1,)), ((), ()))
TN = (((0,), (0,)), ((), ()))


def act(gate, up):
    return jax.nn.gelu(gate) * up


def dot(a, b, dims):
    return lax.dot_general(a, b, dims, preferred_element_type=jnp.float32)


def kernel(
    n, x, dy, gate, up, wg, wu, wd, dx, dwg, dwu, dwd, dg, du, hid, go00, go01, go10, go11,
    wv, wdv, slot, own, dyv, guv, dblk, acc,
    rs_s, rs_r, ag_s, ag_r, ld, wb, wl, lo, tl, so,
):
    bf16 = jnp.bfloat16
    rows, D = x.shape
    F = gate.shape[1]
    J = CUTS
    B, W = rows // n, D // J
    H = B // 2
    NF = F // FB
    S = n - 1 - TAIL
    onward = ((go00, go01), (go10, go11))
    me = lax.axis_index("tp")
    nbr = (lax.rem(me + 1, n), lax.rem(me + n - 1, n))

    def block(d, t):
        return lax.rem(me + 2 * n - 1 - t, n) if d == 0 else lax.rem(me + 1 + t, n)

    def held(d, a):
        return lax.rem(me + n - a, n) if d == 0 else lax.rem(me + a, n)

    def at(b, d):
        return pl.ds(pl.multiple_of(b * B + d * H, H), H)

    def cut(j):
        return pl.ds(pl.multiple_of(j * W, W), W)

    def remote(src, dst, s, r, d):
        return pltpu.make_async_remote_copy(
            src_ref=src, dst_ref=dst, send_sem=s, recv_sem=r,
            device_id={"tp": nbr[d]}, device_id_type=MESH,
        )

    def rs_copy(d, t, j, first=False):
        src = own.at[d, j] if first else slot.at[d, t - 1, j]
        return remote(src, slot.at[d, t, j], rs_s.at[d, t, j], rs_r.at[d, t, j], d)

    def ag_copy(d, a, j, first=False, last=None):
        ref = dx.at[at(held(d, a), d), cut(j)]
        src = slot.at[d, n - 2, j] if first else ref
        if last is not None:
            h, jh = last
            dst = onward[d][h].at[:, pl.ds(pl.multiple_of(jh * W, W), W)]
        else:
            dst = ref
        return remote(src, dst, ag_s.at[d, a, j], ag_r.at[d, a, j], d)

    def mine(d, j):
        return pltpu.make_async_copy(
            slot.at[d, n - 2, j], dx.at[at(me, d), cut(j)], lo.at[d, j]
        )

    def loads(t, buf):
        out = []
        for d in range(2):
            r, v = at(block(d, t), d), pl.ds(d * H, H)
            out.append((dy.at[r, :], dyv.at[buf, v, :]))
            out.append((gate.at[r, :], guv.at[buf, 0, v, :]))
            out.append((up.at[r, :], guv.at[buf, 1, v, :]))
        return [
            pltpu.make_async_copy(s, v, ld.at[buf, i]) for i, (s, v) in enumerate(out)
        ]

    def stores(t, buf):
        out = []
        for d in range(2):
            r, v = at(block(d, t), d), pl.ds(d * H, H)
            for i, ref in enumerate((dg, du, hid)):
                out.append((dblk.at[buf, v, pl.ds(i * F, F)], ref.at[r, :]))
        return [
            pltpu.make_async_copy(v, s, wb.at[buf, i]) for i, (v, s) in enumerate(out)
        ]

    def down(i):
        r = pl.ds(i * FB, FB)
        return pltpu.make_async_copy(wd.at[r, :], wdv.at[r, :], wl.at[0, i])

    def weights(j):
        r = pl.ds(j * W, W)
        return (
            pltpu.make_async_copy(wg.at[r, :], wv.at[r, pl.ds(0, F)], wl.at[1, j]),
            pltpu.make_async_copy(wu.at[r, :], wv.at[r, pl.ds(F, F)], wl.at[2, j]),
        )

    def gradients(buf, i):
        c = pl.ds(pl.multiple_of(i * FB, FB), FB)
        back_in = dot(dyv[buf], wdv[c, :], NT)
        g, u = guv[buf, 0, :, c].astype(jnp.float32), guv[buf, 1, :, c].astype(jnp.float32)
        h, back = jax.vjp(act, g, u)
        d_g, d_u = back(back_in)
        for k, v in enumerate((d_g, d_u, h)):
            dblk[buf, :, pl.ds(pl.multiple_of(k * F + i * FB, FB), FB)] = v.astype(bf16)

    def term(buf, j):
        return dot(dblk[buf, :, pl.ds(0, 2 * F)], wv[cut(j), :], NT)

    for c in loads(0, 0):
        c.start()
    for i in range(NF):
        down(i).start()

    barrier = pltpu.get_barrier_semaphore()
    for d in range(2):
        pl.semaphore_signal(barrier, inc=1, device_id={"tp": nbr[d]}, device_id_type=MESH)

    for c in loads(0, 0):
        c.wait()
    for i in range(NF):
        down(i).wait()
        for j in range(J):
            if min(j + 1, NF - 1) == i:
                for c in weights(j):
                    c.start()
        gradients(0, i)
    for c in stores(0, 0):
        c.start()
    for c in loads(1, 1):
        c.start()
    for j in range(J):
        for c in weights(j):
            c.wait()
        part = term(0, j).astype(bf16)
        own[0, j] = part[:H]
        own[1, j] = part[H:]
        if j == 0:
            pl.semaphore_wait(barrier, 2)
        for d in range(2):
            rs_copy(d, 0, j, first=True).start()

    def step(t, carry):
        buf = lax.rem(t, 2)
        for c in loads(t, buf):
            c.wait()

        @pl.when(t >= 2)
        def _():
            for c in stores(t - 2, buf):
                c.wait()

        @pl.when(t < n - 1)
        def _():
            for c in loads(t + 1, 1 - buf):
                c.start()

        def hidden_part(i, carry):
            gradients(buf, i)
            return carry

        lax.fori_loop(0, NF, hidden_part, 0)
        for c in stores(t, buf):
            c.start()

        def piece(j, carry):
            acc[...] = term(buf, j)
            for d in range(2):
                here = slot.at[d, t - 1, j]
                remote(here, here, rs_s.at[d, t - 1, j], rs_r.at[d, t - 1, j], d).wait_recv()
                total = slot[d, t - 1, j].astype(jnp.float32) + acc[pl.ds(d * H, H), :]
                slot[d, t - 1, j] = total.astype(bf16)

            @pl.when(t < n - 1)
            def _():
                for d in range(2):
                    rs_copy(d, t, j).start()

            @pl.when(t == n - 1)
            def _():
                for d in range(2):
                    ag_copy(d, 0, j, first=True).start()
                    mine(d, j).start()

            return carry

        lax.fori_loop(0, J, piece, 0)
        return carry

    lax.fori_loop(1, n, step, 0)

    for t in (n - 2, n - 1):
        for c in stores(t, t % 2):
            c.wait()
    top, below = pl.ds(0, rows), pl.ds(rows, rows)
    whole = (
        pltpu.make_async_copy(dg, wv.at[top, pl.ds(0, F)], wl.at[0, 0]),
        pltpu.make_async_copy(du, wv.at[top, pl.ds(F, F)], wl.at[1, 0]),
        pltpu.make_async_copy(hid, wv.at[below, pl.ds(0, F)], wl.at[2, 0]),
    )
    NX = D // TW
    U, K = 3 * NX, S * J

    def tile_cols(s):
        return pl.ds(pl.multiple_of(F + s * TW, FB), TW)

    def tile(T, start):
        s = lax.rem(T, 2)
        for ref, first in ((x, 0), (dy, NX)):
            @pl.when((T >= first) & (T < first + NX))
            def _():
                cols = pl.ds(pl.multiple_of((T - first) * TW, TW), TW)
                c = pltpu.make_async_copy(ref.at[:, cols], wv.at[below, tile_cols(s)], tl.at[s])
                c.start() if start else c.wait()

    def out_x(i, g, p):
        return pltpu.make_async_copy(
            wdv.at[pl.ds(0, TW), pl.ds(pl.multiple_of(p * F, FB), F)],
            (dwg, dwu)[g].at[pl.ds(pl.multiple_of(i * TW, TW), TW), :], so.at[0, p],
        )

    def out_y(i, p):
        return pltpu.make_async_copy(
            wdv.at[:, pl.ds(pl.multiple_of(2 * F + p * TW, TW), TW)],
            dwd.at[:, pl.ds(pl.multiple_of(i * TW, TW), TW)], so.at[1, p],
        )

    def unit_x(k):
        i, g = k // 2, lax.rem(k, 2)

        @pl.when(g == 0)
        def _():
            tile(i, False)
            tile(i + 1, True)

        @pl.when(k >= 2)
        def _():
            out_x(0, 0, g).wait()

        half = pl.ds(pl.multiple_of(g * F, FB), F)
        wdv[pl.ds(0, TW), half] = dot(
            wv[below, tile_cols(lax.rem(i, 2))], wv[top, half], TN
        ).astype(bf16)
        for v in range(2):
            @pl.when(g == v)
            def _():
                out_x(i, v, v).start()

    def unit_y(k):
        i = k - 2 * NX
        s = lax.rem(i + NX, 2)
        p = lax.rem(i, 2)

        tile(i + NX, False)
        tile(i + NX + 1, True)

        @pl.when(i >= 2)
        def _():
            out_y(0, p).wait()

        wdv[:, pl.ds(pl.multiple_of(2 * F + p * TW, TW), TW)] = dot(
            wv[below, pl.ds(0, F)], wv[below, tile_cols(s)], TN
        ).astype(bf16)
        out_y(i, p).start()

    for c in whole:
        c.start()
    tile(0, True)
    for c in whole:
        c.wait()

    def tick(k, carry):
        a = k // J + 1
        j = lax.rem(k, J)
        for d in range(2):
            ag_copy(d, a - 1, j).wait_recv()

        @pl.when(a < S - 1)
        def _():
            for d in range(2):
                ag_copy(d, a, j).start()

        for h in range(PARTS):
            jh = j - h * (J // PARTS)

            @pl.when((a == S - 1) & (jh >= 0) & (jh < J // PARTS))
            def _():
                for d in range(2):
                    ag_copy(d, a, j, last=(h, jh)).start()

        def unit(u, carry):
            @pl.when(u < 2 * NX)
            def _():
                unit_x(u)

            @pl.when(u >= 2 * NX)
            def _():
                unit_y(u)

            return carry

        @pl.when(k < spread)
        def _():
            lax.fori_loop(k * U // spread, (k + 1) * U // spread, unit, 0)

        return carry

    spread = (S - 1) * J
    lax.fori_loop(0, K, tick, 0)

    for p in range(2):
        out_x(0, p, p).wait()
        out_y(0, p).wait()

    def drain(t, carry):
        def one(j, carry):
            for d in range(2):
                remote(slot.at[d, 0, j], slot.at[d, t, j], rs_s.at[d, t, j], rs_r.at[d, t, j], d).wait_send()

            @pl.when(t < S)
            def _():
                for d in range(2):
                    ag_copy(d, t, j).wait_send()

            return carry

        return lax.fori_loop(0, J, one, carry)

    lax.fori_loop(0, n - 1, drain, 0)
    for d in range(2):
        for j in range(J):
            mine(d, j).wait()


def carry_over(moves, buf, fill, drain):
    total, depth = len(moves), buf.shape[0]
    ahead = depth // 2

    def read(i):
        return pltpu.make_async_copy(moves[i][0], buf.at[i % depth], fill.at[i % depth])

    def write(i):
        return pltpu.make_async_copy(buf.at[i % depth], moves[i][1], drain.at[i % depth])

    for i in range(total + ahead):
        if i < total:
            if i >= depth:
                write(i - depth).wait()
            read(i).start()
        if i >= ahead:
            read(i - ahead).wait()
            write(i - ahead).start()
    for i in range(max(0, total - depth), total):
        write(i).wait()


def copied(arrays, tokens=None):
    k, depth = len(arrays), 12
    rows = arrays[0].shape[0] // (32 if tokens else 16)

    def body(*refs):
        moves = []
        for src, dst in zip(refs[:k], refs[k:2 * k]):
            if tokens is None:
                starts = [i * rows for i in range(src.shape[0] // rows)]
            else:
                n, steps = tokens
                me = lax.axis_index("tp")
                B = src.shape[0] // n
                starts = []
                for a in range(steps):
                    for d in range(2):
                        b = lax.rem(me + n - a, n) if d == 0 else lax.rem(me + a, n)
                        for q in range(B // 2 // rows):
                            starts.append(pl.multiple_of(b * B + d * (B // 2) + q * rows, rows))
            for r in starts:
                moves.append((src.at[pl.ds(r, rows), :], dst.at[pl.ds(r, rows), :]))
        carry_over(moves, *refs[2 * k:])

    any_ = pl.BlockSpec(memory_space=pl.ANY)
    return pl.pallas_call(
        body,
        out_shape=tuple(jax.ShapeDtypeStruct(a.shape, a.dtype) for a in arrays),
        in_specs=[any_] * k,
        out_specs=[any_] * k,
        scratch_shapes=[
            pltpu.VMEM((depth, rows, arrays[0].shape[1]), arrays[0].dtype),
            pltpu.SemaphoreType.DMA((depth,)),
            pltpu.SemaphoreType.DMA((depth,)),
        ],
        compiler_params=pltpu.CompilerParams(vmem_limit_bytes=58 << 20),
        cost_estimate=pl.CostEstimate(
            flops=COPY_FLOPS * k * arrays[0].size, bytes_accessed=4 * k * arrays[0].size, transcendentals=0
        ),
    )(*arrays)


def place(n, steps, base, *refs):
    blocks, out, sems = refs[:-2], refs[-2], refs[-1]
    me = lax.axis_index("tp")
    H, width = blocks[0].shape
    moves = []
    for i, block in enumerate(blocks):
        step, d, h = steps[i // (2 * PARTS)], i // PARTS % 2, i % PARTS
        b = lax.rem(me + n - 1 - step, n) if d == 0 else lax.rem(me + 1 + step, n)
        for q in range(4):
            r = pl.ds(pl.multiple_of((2 * b + d) * H + q * (H // 4), H // 4), H // 4)
            src = block.at[pl.ds(q * (H // 4), H // 4), :]
            moves.append(pltpu.make_async_copy(src, out.at[r, pl.ds(h * width, width)], sems.at[i, q]))
    for c in moves:
        c.start()
    for c in moves:
        c.wait()


def placed(n, steps, base, blocks):
    any_, vmem = pl.BlockSpec(memory_space=pl.ANY), pl.BlockSpec(memory_space=pltpu.VMEM)
    return pl.pallas_call(
        functools.partial(place, n, steps),
        out_shape=jax.ShapeDtypeStruct(base.shape, base.dtype),
        in_specs=[any_, *[vmem] * len(blocks)],
        out_specs=any_,
        scratch_shapes=[pltpu.SemaphoreType.DMA((len(blocks), 4))],
        input_output_aliases={0: 0},
        compiler_params=pltpu.CompilerParams(vmem_limit_bytes=56 << 20),
        cost_estimate=pl.CostEstimate(
            flops=COPY_FLOPS * base.size // 8, bytes_accessed=base.size // 2, transcendentals=0
        ),
    )(base, *blocks)


def solution(mesh):
    n = mesh.shape["tp"]

    def step(x, dy, gate, up, w_gate, w_up, w_down):
        rows, D = x.shape
        F = gate.shape[1]
        J, B, W = CUTS, rows // n, D // CUTS
        H = B // 2
        bf16 = jnp.bfloat16
        any_ = pl.BlockSpec(memory_space=pl.ANY)
        like = lambda *s: jax.ShapeDtypeStruct(s, bf16)
        dma = pltpu.SemaphoreType.DMA
        out = pl.pallas_call(
            functools.partial(kernel, n),
            out_shape=(
                like(rows, D), like(D, F), like(D, F), like(F, D),
                like(rows, F), like(rows, F), like(rows, F),
                *[like(H, D // PARTS)] * (2 * PARTS),
            ),
            in_specs=[any_] * 7,
            out_specs=[any_] * (7 + 2 * PARTS),
            scratch_shapes=[
                pltpu.VMEM((D, 2 * F), bf16),
                pltpu.VMEM((F, D), bf16),
                pltpu.VMEM((2, n - 1, J, H, W), bf16),
                pltpu.VMEM((2, J, H, W), bf16),
                pltpu.VMEM((2, B, D), bf16),
                pltpu.VMEM((2, 2, B, F), bf16),
                pltpu.VMEM((2, B, 3 * F), bf16),
                pltpu.VMEM((B, W), jnp.float32),
                dma((2, n - 1, J)), dma((2, n - 1, J)),
                dma((2, n - 1, J)), dma((2, n - 1, J)),
                dma((2, 6)), dma((2, 6)), dma((3, max(J, F // FB))),
                dma((2, J)), dma((2,)), dma((2, 2)),
            ],
            compiler_params=pltpu.CompilerParams(
                collective_id=0, has_side_effects=True, vmem_limit_bytes=67043328
            ),
            name="mlp_back",
        )(x, dy, gate, up, w_gate, w_up, w_down)

        def hop(d, a):
            by = 1 if d == 0 else n - 1
            return lax.ppermute(a, "tp", [(q, (q + by) % n) for q in range(n)])

        S = n - 1 - TAIL
        dwg, dwu = copied(out[1:3])
        (dwd,) = copied(out[3:4])
        (dx,) = copied(out[:1], (n, S))
        onward = {(d, h): out[7 + d * PARTS + h] for h in range(PARTS) for d in range(2)}
        arrived = [onward]
        for _ in range(TAIL):
            onward = {(d, h): hop(d, a) for (d, h), a in onward.items()}
            arrived.append(onward)
        arrived = [[got[d, h] for d in range(2) for h in range(PARTS)] for got in arrived]
        dx = placed(n, (S - 1, S), dx, arrived[0] + arrived[1])
        for k in range(1, TAIL):
            dx = placed(n, (S + k,), dx, arrived[k + 1])
        return dx, dwg, dwu, dwd

    tokens, columns, rows = P("dp", None), P(None, "tp"), P("tp", None)
    return jax.shard_map(
        step,
        mesh=mesh,
        in_specs=(tokens, tokens, P("dp", "tp"), P("dp", "tp"), columns, columns, rows),
        out_specs=(tokens, P("dp", "tp"), P("dp", "tp"), P(("dp", "tp"), None)),
        check_vma=False,
    )
```

time: 382 us -> 353 us (0.924)
  local copies, waits for them, and re-layouts: 41.2 us -> 1.82 us
  starting transfers between devices: 0 us -> 8.46 us
  waiting for transfers between devices: 0 us -> 6.95 us
  Pallas kernels: 339 us -> 333 us
    pallas_call x1, Pallas kernels: 339 us -> 294 us  [step(): pl.pallas_call(functools.partial(kernel, n), out_shape=(like(rows, D), li...]
    unnamed x4 -> x16, local copies, waits for them, and re-layouts: 41.2 us -> 1.82 us
    pallas_call x0 -> x5, Pallas kernels: none -> 38.7 us  [the longest x3 31.3 us: copied(): pl.pallas_call(body, out_shape=tuple((jax.ShapeDtypeStruct(a.shape, a.dty...]
    ppermute x0 -> x8, starting transfers between devices: none -> 8.46 us  [hop(): return lax.ppermute(a, 'tp', [(q, (q + by) % n) for q in range(n)])]
    ppermute x0 -> x8, waiting for transfers between devices: none -> 6.95 us  [hop(): return lax.ppermute(a, 'tp', [(q, (q + by) % n) for q in range(n)])]
  transfers between devices with their start and end apart: 0 -> 8, of which waited for: 0 -> 1; matrix products, arithmetic and copies ran while one was open for 0% -> 0% of each run, Pallas kernels for 0% -> 10%
where the time goes in v2:
time: 353 us; the launch traced here: 351 us
  Pallas kernels  333 us (94%)
  starting transfers between devices  8.46 us (2%)
  waiting for transfers between devices  6.95 us (2%)
    pallas_call x1, Pallas kernels, step(): pl.pallas_call(functools.partial(kernel, n), out_shape=(like(rows, D), li...  294 us
    pallas_call x3, Pallas kernels, copied(): pl.pallas_call(body, out_shape=tuple((jax.ShapeDtypeStruct(a.shape, a.dty...  31.3 us
    ppermute x8, starting transfers between devices, hop(): return lax.ppermute(a, 'tp', [(q, (q + by) % n) for q in range(n)])  8.46 us
    pallas_call x2, Pallas kernels, placed(): pl.pallas_call(functools.partial(place, n, steps), out_shape=jax.ShapeDty...  7.37 us
  transfers between devices with their start and end apart: 8, of which 1 were waited for; matrix products, arithmetic and copies ran while one was open for 0% of the time, Pallas kernels for 10%

profile of v2, /device:TPU:21, one launch (start us, length us, event | category | flops | bytes accessed | tf_op | source)
XLA Modules:
  0.0 350.9 jit_solution(13238983233169845080)
XLA Ops:
  0.6 294.1 %mlp_back.1 = (bf16[2048,4096]{1,0:T(8,128)(2,1)}, bf16[4096,1280]{1,0:T(8,128)(2,1)}, bf16[4096,1280]{1,0:T(8,128)(2,1)}, bf16[1280,4096]{1,0:T(8,128)(2,1)}, b...) custom-call(bf16[2048,4096]{1,0:T(8,128)(2,1)} %x.1, ...), custom_call_target="tpu_custom_call" | custom-call | tf_op jit(solution)/shard_map/mlp_back/pallas_call | solution.py:462
  294.7 0.1 collective-permute-start
  294.9 0.1 collective-permute-start.1
  295.0 2.7 collective-permute-start.2
  297.6 1.3 collective-permute-start.3
  299.0 8.5 %shard_map.106 = bf16[1280,4096]{1,0:T(8,128)(2,1)} custom-call(bf16[1280,4096]{1,0:T(8,128)(2,1)} %get-tuple-element.23.refs_0_), custom_call_target="tpu_custom_call" | custom-call | flops 3145728000 | bytes 20971520 | tf_op jit(solution)/shard_map/pallas_call | solution.py:399
  307.5 14.8 %shard_map.105 = (bf16[4096,1280]{1,0:T(8,128)(2,1)}, bf16[4096,1280]{1,0:T(8,128)(2,1)}) custom-call(bf16[4096,1280]{1,0:T(8,128)(2,1)} %get-tuple-element.19.refs_0_, bf16[4096,1280]{1,0:T(8,128)(2,1)} %get-tuple-element.20.refs_1_), custom_call_target="tpu_custom_call" | custom-call | flops 6291456000 | bytes 41943040 | tf_op jit(solution)/shard_map/pallas_call | solution.py:399
  322.3 0.0 collective-permute-done.refs_4_
  322.3 0.0 copy-start
  322.3 0.2 collective-permute-start.4
  322.5 0.0 collective-permute-done.1.refs_5_
  322.5 0.1 collective-permute-start.5
  322.6 0.0 collective-permute-done.2.refs_6_
  322.6 2.6 collective-permute-start.6
  325.2 0.0 collective-permute-done.3.refs_7_
  325.2 1.3 collective-permute-start.7
  326.5 8.0 %shard_map.102.base = bf16[2048,4096]{1,0:T(8,128)(2,1)} custom-call(bf16[2048,4096]{1,0:T(8,128)(2,1)} %get-tuple-element.14.refs_0_), custom_call_target="tpu_custom_call" | custom-call | flops 5033164800 | bytes 33554432 | tf_op jit(solution)/shard_map/pallas_call | solution.py:399
  334.6 0.0 copy-done
  334.6 0.0 copy-done.1
  334.6 0.0 copy-done.2
  334.6 0.0 copy-done.3
  334.6 4.4 %shard_map.103.base = bf16[2048,4096]{1,0:T(8,128)(2,1)} custom-call(bf16[2048,4096]{1,0:T(8,128)(2,1)} %shard_map.102.base, bf16[128,2048]{1,0:T(8,128)(2,1)} %get-tuple-element.15.refs_0_, bf16[128,2048]{1,0:T(8,128)(2,1)} %get-tuple-element.16.refs_1_, bf16[128,2048]{1,0:T(8,128)(2,1)} %get-tuple-element.17.refs_2_, ...), custom_call_target="tpu_custom_call", output_to_operand_aliasing={{}: (0, {})} | custom-call | flops 629145600 | bytes 4194304 | tf_op jit(solution)/shard_map/pallas_call | solution.py:436
  339.0 0.0 collective-permute-done.4.refs_0_
  339.1 0.0 copy-start.4
  339.1 6.9 %collective-permute-done.5.refs_1_ = bf16[128,2048]{1,0:T(8,128)(2,1)S(1)} collective-permute-done((bf16[128,2048]{1,0:T(8,128)(2,1)S(1)}, bf16[128,2048]{1,0:T(8,128)(2,1)S(1)}, u32[]{:S(2)}, u32[]{:S(2)}) %collective-permute-start.5) | collective-permute-done | bytes 524320 | tf_op jit(solution)/shard_map/ppermute | solution.py:493
  346.0 0.0 collective-permute-done.6.refs_2_
  346.0 0.0 collective-permute-done.7.refs_3_
  346.0 0.0 copy-done.4
  346.0 0.8 copy-done.5
  346.8 0.2 copy-done.6
  347.0 0.8 copy-done.7
  347.8 3.0 shard_map.104
  (6 shorter events, 0.0 us)
Async XLA Ops:
  294.7 27.5 %collective-permute-start = (bf16[128,2048]{1,0:T(8,128)(2,1)}, bf16[128,2048]{1,0:T(8,128)(2,1)S(1)}, u32[]{:S(2)}, u32[]{:S(2)}) collective-permute-start(bf16[128,2048]{1,0:T(8,128)(2,1)} %get-tuple-element.15.refs_0_), channel_id=1, source_target_pairs={{0,1},{1,2},{2,3},{3,4},{4,5},{5,6},{6,7},{7,0},{8,9},{9,10},{10,1... | collective-permute-start | bytes 1572872 | tf_op jit(solution)/shard_map/ppermute | solution.py:493
  294.9 27.6 %collective-permute-start.1 = (bf16[128,2048]{1,0:T(8,128)(2,1)}, bf16[128,2048]{1,0:T(8,128)(2,1)S(1)}, u32[]{:S(2)}, u32[]{:S(2)}) collective-permute-start(bf16[128,2048]{1,0:T(8,128)(2,1)} %get-tuple-element.16.refs_1_), channel_id=1, source_target_pairs={{0,1},{1,2},{2,3},{3,4},{4,5},{5,6},{6,7},{7,0},{8,9},{9,10},{10,1... | collective-permute-start | bytes 1572872 | tf_op jit(solution)/shard_map/ppermute | solution.py:493
  295.0 27.7 %collective-permute-start.2 = (bf16[128,2048]{1,0:T(8,128)(2,1)}, bf16[128,2048]{1,0:T(8,128)(2,1)S(1)}, u32[]{:S(2)}, u32[]{:S(2)}) collective-permute-start(bf16[128,2048]{1,0:T(8,128)(2,1)} %get-tuple-element.17.refs_2_), channel_id=1, source_target_pairs={{0,7},{1,0},{2,1},{3,2},{4,3},{5,4},{6,5},{7,6},{8,15},{9,8},{10,9... | collective-permute-start | bytes 1572872 | tf_op jit(solution)/shard_map/ppermute | solution.py:493
  297.6 27.6 %collective-permute-start.3 = (bf16[128,2048]{1,0:T(8,128)(2,1)}, bf16[128,2048]{1,0:T(8,128)(2,1)S(1)}, u32[]{:S(2)}, u32[]{:S(2)}) collective-permute-start(bf16[128,2048]{1,0:T(8,128)(2,1)} %get-tuple-element.18.refs_3_), channel_id=1, source_target_pairs={{0,7},{1,0},{2,1},{3,2},{4,3},{5,4},{6,5},{7,6},{8,15},{9,8},{10,9... | collective-permute-start | bytes 1572872 | tf_op jit(solution)/shard_map/ppermute | solution.py:493
  322.3 12.3 %copy-start = (bf16[128,2048]{1,0:T(8,128)(2,1)}, bf16[128,2048]{1,0:T(8,128)(2,1)S(1)}, u32[]{:S(2)}) copy-start(bf16[128,2048]{1,0:T(8,128)(2,1)S(1)} %collective-permute-done.refs_4_) | copy-start | bytes 1572868
  322.3 16.8 %collective-permute-start.4 = (bf16[128,2048]{1,0:T(8,128)(2,1)S(1)}, bf16[128,2048]{1,0:T(8,128)(2,1)S(1)}, u32[]{:S(2)}, u32[]{:S(2)}) collective-permute-start(bf16[128,2048]{1,0:T(8,128)(2,1)S(1)} %collective-permute-done.refs_4_), channel_id=1, source_target_pairs={{0,1},{1,2},{2,3},{3,4},{4,5},{5,6},{6,7},{7,0},{8,9},{9,10},{10,1... | collective-permute-start | bytes 1572872 | tf_op jit(solution)/shard_map/ppermute | solution.py:493
  322.5 12.1 %copy-start.1 = (bf16[128,2048]{1,0:T(8,128)(2,1)}, bf16[128,2048]{1,0:T(8,128)(2,1)S(1)}, u32[]{:S(2)}) copy-start(bf16[128,2048]{1,0:T(8,128)(2,1)S(1)} %collective-permute-done.1.refs_5_) | copy-start | bytes 1572868
  322.5 23.5 %collective-permute-start.5 = (bf16[128,2048]{1,0:T(8,128)(2,1)S(1)}, bf16[128,2048]{1,0:T(8,128)(2,1)S(1)}, u32[]{:S(2)}, u32[]{:S(2)}) collective-permute-start(bf16[128,2048]{1,0:T(8,128)(2,1)S(1)} %collective-permute-done.1.refs_5_), channel_id=1, source_target_pairs={{0,1},{1,2},{2,3},{3,4},{4,5},{5,6},{6,7},{7,0},{8,9},{9,10},{10,1... | collective-permute-start | bytes 1572872 | tf_op jit(solution)/shard_map/ppermute | solution.py:493
  322.6 12.0 %copy-start.2 = (bf16[128,2048]{1,0:T(8,128)(2,1)}, bf16[128,2048]{1,0:T(8,128)(2,1)S(1)}, u32[]{:S(2)}) copy-start(bf16[128,2048]{1,0:T(8,128)(2,1)S(1)} %collective-permute-done.2.refs_6_) | copy-start | bytes 1572868
  322.6 23.4 %collective-permute-start.6 = (bf16[128,2048]{1,0:T(8,128)(2,1)S(1)}, bf16[128,2048]{1,0:T(8,128)(2,1)S(1)}, u32[]{:S(2)}, u32[]{:S(2)}) collective-permute-start(bf16[128,2048]{1,0:T(8,128)(2,1)S(1)} %collective-permute-done.2.refs_6_), channel_id=1, source_target_pairs={{0,7},{1,0},{2,1},{3,2},{4,3},{5,4},{6,5},{7,6},{8,15},{9,8},{10,9... | collective-permute-start | bytes 1572872 | tf_op jit(solution)/shard_map/ppermute | solution.py:493
  325.2 9.4 %copy-start.3 = (bf16[128,2048]{1,0:T(8,128)(2,1)}, bf16[128,2048]{1,0:T(8,128)(2,1)S(1)}, u32[]{:S(2)}) copy-start(bf16[128,2048]{1,0:T(8,128)(2,1)S(1)} %collective-permute-done.3.refs_7_) | copy-start | bytes 1572868
  325.2 20.8 %collective-permute-start.7 = (bf16[128,2048]{1,0:T(8,128)(2,1)S(1)}, bf16[128,2048]{1,0:T(8,128)(2,1)S(1)}, u32[]{:S(2)}, u32[]{:S(2)}) collective-permute-start(bf16[128,2048]{1,0:T(8,128)(2,1)S(1)} %collective-permute-done.3.refs_7_), channel_id=1, source_target_pairs={{0,7},{1,0},{2,1},{3,2},{4,3},{5,4},{6,5},{7,6},{8,15},{9,8},{10,9... | collective-permute-start | bytes 1572872 | tf_op jit(solution)/shard_map/ppermute | solution.py:493
  339.1 7.0 %copy-start.4 = (bf16[128,2048]{1,0:T(8,128)(2,1)}, bf16[128,2048]{1,0:T(8,128)(2,1)S(1)}, u32[]{:S(2)}) copy-start(bf16[128,2048]{1,0:T(8,128)(2,1)S(1)} %collective-permute-done.4.refs_0_) | copy-start | bytes 1572868
  346.0 0.8 copy-start.5
  346.0 1.0 copy-start.6
  347.0 0.8 copy-start.7

commit v3 on v2

--- a/solution.py
+++ b/solution.py
@@ -284,8 +284,6 @@
     for c in whole:
         c.start()
     tile(0, True)
-    for c in whole:
-        c.wait()
 
     def tick(k, carry):
         a = k // J + 1
@@ -317,13 +315,18 @@
 
             return carry
 
+        @pl.when(k == 0)
+        def _():
+            for c in whole:
+                c.wait()
+
         @pl.when(k < spread)
         def _():
             lax.fori_loop(k * U // spread, (k + 1) * U // spread, unit, 0)
 
         return carry
 
-    spread = (S - 1) * J
+    spread = S * J - 2
     lax.fori_loop(0, K, tick, 0)
 
     for p in range(2):
@@ -395,31 +398,31 @@
                 moves.append((src.at[pl.ds(r, rows), :], dst.at[pl.ds(r, rows), :]))
         carry_over(moves, *refs[2 * k:])
 
-    any_ = pl.BlockSpec(memory_space=pl.ANY)
+    hbm = pl.BlockSpec(memory_space=pltpu.HBM)
     return pl.pallas_call(
         body,
         out_shape=tuple(jax.ShapeDtypeStruct(a.shape, a.dtype) for a in arrays),
-        in_specs=[any_] * k,
-        out_specs=[any_] * k,
+        in_specs=[hbm] * k,
+        out_specs=[hbm] * k,
         scratch_shapes=[
             pltpu.VMEM((depth, rows, arrays[0].shape[1]), arrays[0].dtype),
             pltpu.SemaphoreType.DMA((depth,)),
             pltpu.SemaphoreType.DMA((depth,)),
         ],
-        compiler_params=pltpu.CompilerParams(vmem_limit_bytes=58 << 20),
+        compiler_params=pltpu.CompilerParams(vmem_limit_bytes=56 << 20),
         cost_estimate=pl.CostEstimate(
             flops=COPY_FLOPS * k * arrays[0].size, bytes_accessed=4 * k * arrays[0].size, transcendentals=0
         ),
     )(*arrays)
 
 
-def place(n, steps, base, *refs):
+def place(n, whence, base, *refs):
     blocks, out, sems = refs[:-2], refs[-2], refs[-1]
     me = lax.axis_index("tp")
     H, width = blocks[0].shape
     moves = []
     for i, block in enumerate(blocks):
-        step, d, h = steps[i // (2 * PARTS)], i // PARTS % 2, i % PARTS
+        step, d, h = whence[i]
         b = lax.rem(me + n - 1 - step, n) if d == 0 else lax.rem(me + 1 + step, n)
         for q in range(4):
             r = pl.ds(pl.multiple_of((2 * b + d) * H + q * (H // 4), H // 4), H // 4)
@@ -431,16 +434,17 @@
         c.wait()
 
 
-def placed(n, steps, base, blocks):
-    any_, vmem = pl.BlockSpec(memory_space=pl.ANY), pl.BlockSpec(memory_space=pltpu.VMEM)
+def placed(n, base, arrived):
+    hbm, vmem = pl.BlockSpec(memory_space=pltpu.HBM), pl.BlockSpec(memory_space=pltpu.VMEM)
+    whence, blocks = list(arrived), list(arrived.values())
     return pl.pallas_call(
-        functools.partial(place, n, steps),
+        functools.partial(place, n, whence),
         out_shape=jax.ShapeDtypeStruct(base.shape, base.dtype),
-        in_specs=[any_, *[vmem] * len(blocks)],
-        out_specs=any_,
+        in_specs=[hbm, *[vmem] * len(blocks)],
+        out_specs=hbm,
         scratch_shapes=[pltpu.SemaphoreType.DMA((len(blocks), 4))],
         input_output_aliases={0: 0},
-        compiler_params=pltpu.CompilerParams(vmem_limit_bytes=56 << 20),
+        compiler_params=pltpu.CompilerParams(vmem_limit_bytes=16 << 20),
         cost_estimate=pl.CostEstimate(
             flops=COPY_FLOPS * base.size // 8, bytes_accessed=base.size // 2, transcendentals=0
         ),
@@ -497,14 +501,15 @@
         (dwd,) = copied(out[3:4])
         (dx,) = copied(out[:1], (n, S))
         onward = {(d, h): out[7 + d * PARTS + h] for h in range(PARTS) for d in range(2)}
-        arrived = [onward]
-        for _ in range(TAIL):
+        arrived = {(S - 1, *i): a for i, a in onward.items()}
+        for k in range(TAIL):
             onward = {(d, h): hop(d, a) for (d, h), a in onward.items()}
-            arrived.append(onward)
-        arrived = [[got[d, h] for d in range(2) for h in range(PARTS)] for got in arrived]
-        dx = placed(n, (S - 1, S), dx, arrived[0] + arrived[1])
-        for k in range(1, TAIL):
-            dx = placed(n, (S + k,), dx, arrived[k + 1])
+            arrived |= {(S + k, *i): a for i, a in onward.items()}
+        for now in (
+            lambda step, h: step < n - 2,
+            *[lambda step, h, part=part: step == n - 2 and h == part for part in range(PARTS)],
+        ):
+            dx = placed(n, dx, {i: a for i, a in arrived.items() if now(i[0], i[2])})
         return dx, dwg, dwu, dwd
 
     tokens, columns, rows = P("dp", None), P(None, "tp"), P("tp", None)

time: 353 us -> 350 us (level)
    pallas_call x2 -> x3, Pallas kernels: 7.37 us -> 4.34 us  [placed(): pl.pallas_call(functools.partial(place, n, whence), out_shape=jax.ShapeDt...]
where the time goes in v3:
time: 350 us; the launch traced here: 348 us
  Pallas kernels  331 us (95%)
  starting transfers between devices  10.9 us (3%)
  waiting for transfers between devices  5.99 us (2%)
    pallas_call x1, Pallas kernels, step(): pl.pallas_call(functools.partial(kernel, n), out_shape=(like(rows, D), li...  294 us
    pallas_call x3, Pallas kernels, copied(): pl.pallas_call(body, out_shape=tuple((jax.ShapeDtypeStruct(a.shape, a.dty...  32.1 us
    ppermute x8, starting transfers between devices, hop(): return lax.ppermute(a, 'tp', [(q, (q + by) % n) for q in range(n)])  10.9 us
  transfers between devices with their start and end apart: 8, of which 1 were waited for; matrix products, arithmetic and copies ran while one was open for 0% of the time, Pallas kernels for 10%

profile of v3, /device:TPU:21, one launch (start us, length us, event | category | flops | bytes accessed | tf_op | source)
XLA Modules:
  0.0 348.4 jit_solution(7358326590754323042)
XLA Ops:
  0.6 294.1 %mlp_back.1 = (bf16[2048,4096]{1,0:T(8,128)(2,1)}, bf16[4096,1280]{1,0:T(8,128)(2,1)}, bf16[4096,1280]{1,0:T(8,128)(2,1)}, bf16[1280,4096]{1,0:T(8,128)(2,1)}, b...) custom-call(bf16[2048,4096]{1,0:T(8,128)(2,1)} %x.1, ...), custom_call_target="tpu_custom_call" | custom-call | tf_op jit(solution)/shard_map/mlp_back/pallas_call | solution.py:466
  294.7 0.1 collective-permute-start
  294.9 2.7 collective-permute-start.1
  297.5 0.0 collective-permute-start.2
  297.5 2.7 collective-permute-start.3
  300.2 8.5 %shard_map.107 = bf16[1280,4096]{1,0:T(8,128)(2,1)} custom-call(bf16[1280,4096]{1,0:T(8,128)(2,1)} %get-tuple-element.23.refs_0_), custom_call_target="tpu_custom_call" | custom-call | flops 3145728000 | bytes 20971520 | tf_op jit(solution)/shard_map/pallas_call | solution.py:402
  308.7 14.8 %shard_map.106 = (bf16[4096,1280]{1,0:T(8,128)(2,1)}, bf16[4096,1280]{1,0:T(8,128)(2,1)}) custom-call(bf16[4096,1280]{1,0:T(8,128)(2,1)} %get-tuple-element.19.refs_0_, bf16[4096,1280]{1,0:T(8,128)(2,1)} %get-tuple-element.20.refs_1_), custom_call_target="tpu_custom_call" | custom-call | flops 6291456000 | bytes 41943040 | tf_op jit(solution)/shard_map/pallas_call | solution.py:402
  323.5 0.0 collective-permute-done.refs_4_
  323.5 0.1 collective-permute-start.4
  323.6 0.0 collective-permute-done.1.refs_5_
  323.6 2.6 collective-permute-start.5
  326.3 0.0 collective-permute-done.2.refs_6_
  326.3 0.0 collective-permute-start.6
  326.3 0.0 collective-permute-done.3.refs_7_
  326.3 2.7 collective-permute-start.7
  328.9 0.0 copy-start
  328.9 0.0 copy-start.1
  328.9 0.0 copy-start.2
  328.9 0.0 copy-start.3
  329.0 8.9 %shard_map.102.base = bf16[2048,4096]{1,0:T(8,128)(2,1)} custom-call(bf16[2048,4096]{1,0:T(8,128)(2,1)} %get-tuple-element.14.refs_0_), custom_call_target="tpu_custom_call" | custom-call | flops 5033164800 | bytes 33554432 | tf_op jit(solution)/shard_map/pallas_call | solution.py:402
  337.8 0.0 copy-done
  337.8 0.0 copy-done.1
  337.8 0.0 copy-done.2
  337.9 0.0 copy-done.3
  337.9 2.3 shard_map.103.base
  340.2 0.0 collective-permute-done.4.refs_0_
  340.2 0.0 collective-permute-done.5.refs_1_
  340.2 1.0 shard_map.104.base
  341.2 6.0 %collective-permute-done.6.refs_0_ = bf16[128,2048]{1,0:T(8,128)(2,1)S(1)} collective-permute-done((bf16[128,2048]{1,0:T(8,128)(2,1)S(1)}, bf16[128,2048]{1,0:T(8,128)(2,1)S(1)}, u32[]{:S(2)}, u32[]{:S(2)}) %collective-permute-start.6) | collective-permute-done | bytes 524320 | tf_op jit(solution)/shard_map/ppermute | solution.py:497
  347.2 0.0 collective-permute-done.7.refs_1_
  347.2 1.0 shard_map.105
Async XLA Ops:
  294.7 28.7 %collective-permute-start = (bf16[128,2048]{1,0:T(8,128)(2,1)}, bf16[128,2048]{1,0:T(8,128)(2,1)S(1)}, u32[]{:S(2)}, u32[]{:S(2)}) collective-permute-start(bf16[128,2048]{1,0:T(8,128)(2,1)} %get-tuple-element.15.refs_0_), channel_id=1, source_target_pairs={{0,1},{1,2},{2,3},{3,4},{4,5},{5,6},{6,7},{7,0},{8,9},{9,10},{10,1... | collective-permute-start | bytes 1572872 | tf_op jit(solution)/shard_map/ppermute | solution.py:497
  294.9 28.7 %collective-permute-start.1 = (bf16[128,2048]{1,0:T(8,128)(2,1)}, bf16[128,2048]{1,0:T(8,128)(2,1)S(1)}, u32[]{:S(2)}, u32[]{:S(2)}) collective-permute-start(bf16[128,2048]{1,0:T(8,128)(2,1)} %get-tuple-element.16.refs_1_), channel_id=1, source_target_pairs={{0,7},{1,0},{2,1},{3,2},{4,3},{5,4},{6,5},{7,6},{8,15},{9,8},{10,9... | collective-permute-start | bytes 1572872 | tf_op jit(solution)/shard_map/ppermute | solution.py:497
  297.5 28.7 %collective-permute-start.2 = (bf16[128,2048]{1,0:T(8,128)(2,1)}, bf16[128,2048]{1,0:T(8,128)(2,1)S(1)}, u32[]{:S(2)}, u32[]{:S(2)}) collective-permute-start(bf16[128,2048]{1,0:T(8,128)(2,1)} %get-tuple-element.17.refs_2_), channel_id=1, source_target_pairs={{0,1},{1,2},{2,3},{3,4},{4,5},{5,6},{6,7},{7,0},{8,9},{9,10},{10,1... | collective-permute-start | bytes 1572872 | tf_op jit(solution)/shard_map/ppermute | solution.py:497
  297.5 28.7 %collective-permute-start.3 = (bf16[128,2048]{1,0:T(8,128)(2,1)}, bf16[128,2048]{1,0:T(8,128)(2,1)S(1)}, u32[]{:S(2)}, u32[]{:S(2)}) collective-permute-start(bf16[128,2048]{1,0:T(8,128)(2,1)} %get-tuple-element.18.refs_3_), channel_id=1, source_target_pairs={{0,7},{1,0},{2,1},{3,2},{4,3},{5,4},{6,5},{7,6},{8,15},{9,8},{10,9... | collective-permute-start | bytes 1572872 | tf_op jit(solution)/shard_map/ppermute | solution.py:497
  323.5 16.7 %collective-permute-start.4 = (bf16[128,2048]{1,0:T(8,128)(2,1)S(1)}, bf16[128,2048]{1,0:T(8,128)(2,1)S(1)}, u32[]{:S(2)}, u32[]{:S(2)}) collective-permute-start(bf16[128,2048]{1,0:T(8,128)(2,1)S(1)} %collective-permute-done.refs_4_), channel_id=1, source_target_pairs={{0,1},{1,2},{2,3},{3,4},{4,5},{5,6},{6,7},{7,0},{8,9},{9,10},{10,1... | collective-permute-start | bytes 1572872 | tf_op jit(solution)/shard_map/ppermute | solution.py:497
  323.6 16.6 %collective-permute-start.5 = (bf16[128,2048]{1,0:T(8,128)(2,1)S(1)}, bf16[128,2048]{1,0:T(8,128)(2,1)S(1)}, u32[]{:S(2)}, u32[]{:S(2)}) collective-permute-start(bf16[128,2048]{1,0:T(8,128)(2,1)S(1)} %collective-permute-done.1.refs_5_), channel_id=1, source_target_pairs={{0,7},{1,0},{2,1},{3,2},{4,3},{5,4},{6,5},{7,6},{8,15},{9,8},{10,9... | collective-permute-start | bytes 1572872 | tf_op jit(solution)/shard_map/ppermute | solution.py:497
  326.3 20.9 %collective-permute-start.6 = (bf16[128,2048]{1,0:T(8,128)(2,1)S(1)}, bf16[128,2048]{1,0:T(8,128)(2,1)S(1)}, u32[]{:S(2)}, u32[]{:S(2)}) collective-permute-start(bf16[128,2048]{1,0:T(8,128)(2,1)S(1)} %collective-permute-done.2.refs_6_), channel_id=1, source_target_pairs={{0,1},{1,2},{2,3},{3,4},{4,5},{5,6},{6,7},{7,0},{8,9},{9,10},{10,1... | collective-permute-start | bytes 1572872 | tf_op jit(solution)/shard_map/ppermute | solution.py:497
  326.3 20.9 %collective-permute-start.7 = (bf16[128,2048]{1,0:T(8,128)(2,1)S(1)}, bf16[128,2048]{1,0:T(8,128)(2,1)S(1)}, u32[]{:S(2)}, u32[]{:S(2)}) collective-permute-start(bf16[128,2048]{1,0:T(8,128)(2,1)S(1)} %collective-permute-done.3.refs_7_), channel_id=1, source_target_pairs={{0,7},{1,0},{2,1},{3,2},{4,3},{5,4},{6,5},{7,6},{8,15},{9,8},{10,9... | collective-permute-start | bytes 1572872 | tf_op jit(solution)/shard_map/ppermute | solution.py:497
  328.9 8.9 %copy-start = (bf16[128,2048]{1,0:T(8,128)(2,1)S(1)}, bf16[128,2048]{1,0:T(8,128)(2,1)}, u32[]{:S(2)}) copy-start(bf16[128,2048]{1,0:T(8,128)(2,1)} %get-tuple-element.15.refs_0_) | copy-start | bytes 1572868
  328.9 8.9 %copy-start.1 = (bf16[128,2048]{1,0:T(8,128)(2,1)S(1)}, bf16[128,2048]{1,0:T(8,128)(2,1)}, u32[]{:S(2)}) copy-start(bf16[128,2048]{1,0:T(8,128)(2,1)} %get-tuple-element.17.refs_2_) | copy-start | bytes 1572868
  328.9 8.9 %copy-start.2 = (bf16[128,2048]{1,0:T(8,128)(2,1)S(1)}, bf16[128,2048]{1,0:T(8,128)(2,1)}, u32[]{:S(2)}) copy-start(bf16[128,2048]{1,0:T(8,128)(2,1)} %get-tuple-element.16.refs_1_) | copy-start | bytes 1572868
  328.9 8.9 %copy-start.3 = (bf16[128,2048]{1,0:T(8,128)(2,1)S(1)}, bf16[128,2048]{1,0:T(8,128)(2,1)}, u32[]{:S(2)}) copy-start(bf16[128,2048]{1,0:T(8,128)(2,1)} %get-tuple-element.18.refs_3_) | copy-start | bytes 1572868
